TPU v7x, 32 devices: a whole 2x2x4 slice. The times are simulated.
32 devices in a mesh: fsdp: 32 (over z, y, x, core).
Axes of the slice: x: 2, y: 2, z: 4, core: 2. Of those that a mesh axis runs over, the one named last changes fastest.
Arguments:
- resid_in: bfloat16 [96, 257, 1408], P('fsdp')
- grad_out: bfloat16 [96, 257, 1408], P('fsdp')
- ln1_gain: float32 [1408], P('fsdp')
- ln1_bias: float32 [1408], P('fsdp')
- qkv_weight: float32 [1408, 4224], P('fsdp')
- qkv_bias: float32 [4224], P('fsdp')
- out_weight: float32 [1408, 1408], P('fsdp')
- out_bias: float32 [1408], P('fsdp')
- ln2_gain: float32 [1408], P('fsdp')
- ln2_bias: float32 [1408], P('fsdp')
- fc_weight: float32 [1408, 6144], P('fsdp')
- fc_bias: float32 [6144], P('fsdp')
- proj_weight: float32 [6144, 1408], P('fsdp')
- proj_bias: float32 [1408], P('fsdp')
Outputs:
- output 1: bfloat16 [96, 257, 1408], P('fsdp')
- output 2: bfloat16 [96, 257, 1408], P('fsdp')
- output 3: float32 [1408], P('fsdp')
- output 4: float32 [1408], P('fsdp')
- output 5: float32 [1408, 4224], P('fsdp')
- output 6: float32 [4224], P('fsdp')
- output 7: float32 [1408, 1408], P('fsdp')
- output 8: float32 [1408], P('fsdp')
- output 9: float32 [1408], P('fsdp')
- output 10: float32 [1408], P('fsdp')
- output 11: float32 [1408, 6144], P('fsdp')
- output 12: float32 [6144], P('fsdp')
- output 13: float32 [6144, 1408], P('fsdp')
- output 14: float32 [1408], P('fsdp')
All inputs are finite; a program needn't handle non-finite values.
Results may differ from a plain program's by a relative error of at most 0.02.
Values are sent between devices in bfloat16 or wider.
A program may use at most 1 GiB of HBM per device.

v0:
```python
import math
import jax
import jax.numpy as jnp
from jax import lax
from jax.sharding import PartitionSpec as P

HEADS = 16
LN_EPS = 1e-5


def layer_norm_fwd(values, gain, bias):
    mean_val = jnp.mean(values, axis=-1, keepdims=True)
    centered = values - mean_val
    inv_std = lax.rsqrt(jnp.mean(centered * centered, axis=-1, keepdims=True) + LN_EPS)
    x_hat = centered * inv_std
    return x_hat * gain + bias, x_hat, inv_std


def layer_norm_bwd(grad_norm, x_hat, inv_std, gain):
    grad_hat = grad_norm * gain
    grad_vals = inv_std * (grad_hat - jnp.mean(grad_hat, axis=-1, keepdims=True)
                           - x_hat * jnp.mean(grad_hat * x_hat, axis=-1, keepdims=True))
    return grad_vals, jnp.sum(grad_norm * x_hat, axis=(0, 1)), jnp.sum(grad_norm, axis=(0, 1))


def forward_local(full, tokens):
    (ln1_gain, ln1_bias, qkv_weight, qkv_bias, out_weight, out_bias,
     ln2_gain, ln2_bias, fc_weight, fc_bias, proj_weight, proj_bias) = full
    images, seq_len, width = tokens.shape
    head_dim = width // HEADS
    resid = tokens.astype(jnp.float32)
    normed, hat_one, inv_one = layer_norm_fwd(resid, ln1_gain, ln1_bias)
    normed_one = normed.astype(jnp.bfloat16)
    qkv_vals = (jnp.einsum("bsw,wk->bsk", normed_one, qkv_weight, preferred_element_type=jnp.float32) + qkv_bias).astype(jnp.bfloat16)
    qkv_vals = qkv_vals.reshape(images, seq_len, 3, HEADS, head_dim)
    query_heads = qkv_vals[:, :, 0]
    key_heads = qkv_vals[:, :, 1]
    value_heads = qkv_vals[:, :, 2]
    scores = jnp.einsum("bqhd,bkhd->bhqk", query_heads, key_heads, preferred_element_type=jnp.float32) * (head_dim ** -0.5)
    attn_probs = jax.nn.softmax(scores, axis=-1)
    probs_low = attn_probs.astype(jnp.bfloat16)
    mixed = jnp.einsum("bhqk,bkhd->bqhd", probs_low, value_heads, preferred_element_type=jnp.float32).astype(jnp.bfloat16).reshape(images, seq_len, width)
    middle = (resid + jnp.einsum("bsw,wv->bsv", mixed, out_weight, preferred_element_type=jnp.float32) + out_bias).astype(jnp.bfloat16)
    middle_wide = middle.astype(jnp.float32)
    normed, hat_two, inv_two = layer_norm_fwd(middle_wide, ln2_gain, ln2_bias)
    normed_two = normed.astype(jnp.bfloat16)
    pre_act = jnp.einsum("bsw,wf->bsf", normed_two, fc_weight, preferred_element_type=jnp.float32) + fc_bias
    hidden = jax.nn.gelu(pre_act, approximate=False).astype(jnp.bfloat16)
    resid_out = (middle_wide + jnp.einsum("bsf,fw->bsw", hidden, proj_weight, preferred_element_type=jnp.float32) + proj_bias).astype(jnp.bfloat16)
    saved = (hat_one, inv_one, normed_one, query_heads, key_heads, value_heads, attn_probs, probs_low,
             mixed, hat_two, inv_two, normed_two, pre_act, hidden)
    return resid_out, saved


def backward_local(weights, saved, grad_out):
    (ln1_gain, qkv_weight, out_weight, ln2_gain, fc_weight, proj_weight) = weights
    (hat_one, inv_one, normed_one, query_heads, key_heads, value_heads, attn_probs, probs_low,
     mixed, hat_two, inv_two, normed_two, pre_act, hidden) = saved
    images, seq_len, width = grad_out.shape
    head_dim = width // HEADS
    grad_wide = grad_out.astype(jnp.float32)
    d_proj_weight = jnp.einsum("bsf,bsw->fw", hidden, grad_out, preferred_element_type=jnp.float32)
    d_proj_bias = jnp.sum(grad_wide, axis=(0, 1))
    grad_hidden = jnp.einsum("bsw,fw->bsf", grad_out, proj_weight, preferred_element_type=jnp.float32)
    gauss_cdf = 0.5 * (1.0 + lax.erf(pre_act * (0.5 ** 0.5)))
    gauss_pdf = jnp.exp(-0.5 * pre_act * pre_act) * ((2.0 * math.pi) ** -0.5)
    grad_pre = grad_hidden * (gauss_cdf + pre_act * gauss_pdf)
    grad_pre_low = grad_pre.astype(jnp.bfloat16)
    d_fc_weight = jnp.einsum("bsw,bsf->wf", normed_two, grad_pre_low, preferred_element_type=jnp.float32)
    d_fc_bias = jnp.sum(grad_pre, axis=(0, 1))
    grad_norm = jnp.einsum("bsf,wf->bsw", grad_pre_low, fc_weight, preferred_element_type=jnp.float32)
    grad_ln, d_ln2_gain, d_ln2_bias = layer_norm_bwd(grad_norm, hat_two, inv_two, ln2_gain)
    grad_middle = grad_wide + grad_ln
    grad_middle_low = grad_middle.astype(jnp.bfloat16)
    d_out_weight = jnp.einsum("bsw,bsv->wv", mixed, grad_middle_low, preferred_element_type=jnp.float32)
    d_out_bias = jnp.sum(grad_middle, axis=(0, 1))
    grad_mixed = jnp.einsum("bsv,wv->bsw", grad_middle_low, out_weight, preferred_element_type=jnp.float32)
    grad_mixed = grad_mixed.astype(jnp.bfloat16).reshape(images, seq_len, HEADS, head_dim)
    grad_probs = jnp.einsum("bqhd,bkhd->bhqk", grad_mixed, value_heads, preferred_element_type=jnp.float32)
    grad_value = jnp.einsum("bhqk,bqhd->bkhd", probs_low, grad_mixed, preferred_element_type=jnp.float32)
    grad_scores = attn_probs * (grad_probs - jnp.sum(grad_probs * attn_probs, axis=-1, keepdims=True)) * (head_dim ** -0.5)
    grad_scores = grad_scores.astype(jnp.bfloat16)
    grad_query = jnp.einsum("bhqk,bkhd->bqhd", grad_scores, key_heads, preferred_element_type=jnp.float32)
    grad_key = jnp.einsum("bhqk,bqhd->bkhd", grad_scores, query_heads, preferred_element_type=jnp.float32)
    grad_qkv = jnp.stack([grad_query, grad_key, grad_value], axis=2).reshape(images, seq_len, 3 * width)
    grad_qkv_low = grad_qkv.astype(jnp.bfloat16)
    d_qkv_weight = jnp.einsum("bsw,bsk->wk", normed_one, grad_qkv_low, preferred_element_type=jnp.float32)
    d_qkv_bias = jnp.sum(grad_qkv, axis=(0, 1))
    grad_norm = jnp.einsum("bsk,wk->bsw", grad_qkv_low, qkv_weight, preferred_element_type=jnp.float32)
    grad_ln, d_ln1_gain, d_ln1_bias = layer_norm_bwd(grad_norm, hat_one, inv_one, ln1_gain)
    grad_in = (grad_middle + grad_ln).astype(jnp.bfloat16)
    return grad_in, (d_ln1_gain, d_ln1_bias, d_qkv_weight, d_qkv_bias, d_out_weight, d_out_bias,
                     d_ln2_gain, d_ln2_bias, d_fc_weight, d_fc_bias, d_proj_weight, d_proj_bias)


def solution(mesh):
    specs = (P("fsdp"),) * 14

    def gather_bf16(shards):
        return tuple(lax.all_gather(shard.astype(jnp.bfloat16), "fsdp", axis=0, tiled=True) for shard in shards)

    def device_step(resid_in, grad_out, *shards):
        full = gather_bf16(shards)
        resid_out, saved = forward_local(full, resid_in)
        needed, resid_out = lax.optimization_barrier(
            ((shards[0], shards[2], shards[4], shards[6], shards[8], shards[10]), resid_out))
        weights = gather_bf16(needed)
        grad_in, grads = backward_local(weights, saved, grad_out)
        grad_shards = tuple(lax.psum_scatter(grad, "fsdp", scatter_dimension=0, tiled=True) for grad in grads)
        return (resid_out, grad_in) + grad_shards

    return jax.shard_map(device_step, mesh=mesh, in_specs=specs, out_specs=specs, check_vma=False)
```

profile of v0, /device:TPU:1, one launch (start us, length us, event | category | flops | bytes accessed | tf_op | source)
XLA Modules:
  0.0 2182.7 jit_solution(3817602472455872454)
XLA Ops:
  22.6 43.6 %all-reduce.26 = (bf16[4224]{0:T(1024)(128)(2,1)S(1)}, bf16[1408]{0:T(1024)(128)(2,1)S(1)}, bf16[1408]{0:T(1024)(128)(2,1)S(1)}, bf16[1408]{0:T(1024)(128)(2,1)S...) all-reduce(bf16[4224]{0:T(1024)(128)(2,1)S(1)} %dynamic-update-slic, ...), channel_id=1, replica_groups=mesh['fsdp'=32] {'fsdp'}, use_global_device_ids=true, to_apply=%add.2 | all-reduce | flops 18816 | bytes 75264
  82.7 93.4 %all-gather.19.cloned.1.call-done = bf16[32,44,4224]{2,1,0:T(8,128)(2,1)} async-done(((bf16[1,44,4224]{2,1,0:T(8,128)(2,1)}), bf16[32,44,4224]{2,1,0:T(8,128)(2,1)}) %all-gather.19.cloned.1.call-update) | async-done | bytes 11894800 | tf_op jit(solution)/shard_map/all_gather | solution.py:100
  209.4 21.5 reshape.93
  257.4 22.1 %fusion.107 = (f32[3,16,257]{2,1,0:T(8,128)S(1)}, f32[3,16,257,257]{2,3,1,0:T(8,128)}) fusion(f32[3,16,257,257]{2,3,1,0:T(8,128)} %fusion.86), kind=kOutput, calls=%fused_computation.138 | output fusion | flops 12681664 | bytes 25412160 | tf_op jit(solution)/shard_map/sub | solution.py:40
  301.4 19.3 reshape.130
  320.7 29.5 %fusion.60 = (u8[257,6144]{1,0:T(8,128)(4,1)S(1)}, u8[257,6144]{1,0:T(8,128)(4,1)S(1)}, f32[3,257,6144]{2,1,0:T(8,128)}) fusion(f32[6144]{0:T(1024)S(1)} %convert_element_type.166, bf16[1408,6144,1]{1,0,2:T(8,128)(2,1)} %reshape.130, bf16[3,257,1408]{2,1,0:T(8,128)(2,1)S(1)} %copy-done.8, f32[1408]{0:T(1024)S(1)} %convert_element_type.162, ...), kind=kOutput, calls=%fused_computation.80 | convolution fusion | flops 13409133568 | bytes 41620760 | tf_op jit(solution)/shard_map/bsw,wf->bsf/dot_general | solution.py:47
  350.2 47.6 %fusion.7 = bf16[3,257,6144]{2,1,0:T(8,128)(2,1)} fusion(f32[3,257,6144]{2,1,0:T(8,128)} %get-tuple-element.70, f32[6144]{0:T(1024)S(1)} %convert_element_type.166, u8[257,6144]{1,0:T(8,128)(4,1)S(1)} %get-tuple-element.29, u8[257,6144]{1,0:T(8,128)(4,1)S(1)} %get-tuple-element.28), kind=kLoop, calls=%fused_computation.9 | loop fusion | flops 336328704 | bytes 31604736 | tf_op jit(solution)/shard_map/convert_element_type | solution.py:48
  397.8 22.0 %all-gather.15.cloned.1.call-done = bf16[6144,1408]{1,0:T(8,128)(2,1)} async-done(((bf16[192,1408]{1,0:T(8,128)(2,1)}), bf16[6144,1408]{1,0:T(8,128)(2,1)}) %all-gather.15.cloned.1.call-update) | async-done | bytes 17301520 | tf_op jit(solution)/shard_map/all_gather | solution.py:100
  419.8 22.1 %fusion.80 = bf16[3,257,1408]{2,1,0:T(8,128)(2,1)} fusion(bf16[3,257,1408]{2,1,0:T(8,128)(2,1)S(1)} %copy-done.8, bf16[3,257,6144]{2,1,0:T(8,128)(2,1)} %fusion.7, bf16[6144,1408]{1,0:T(8,128)(2,1)} %all-gather.15.cloned.1.call-done, f32[1408]{0:T(1024)S(1)} %convert_element_type.170), kind=kOutput, calls=%fused_computation.100 | convolution fusion | flops 13343801344 | bytes 31123456 | tf_op jit(solution)/shard_map/bsf,fw->bsw/dot_general | solution.py:49
  448.3 37.7 %all-reduce.25 = (bf16[1408]{0:T(1024)(128)(2,1)S(1)}, bf16[1408]{0:T(1024)(128)(2,1)S(1)}) all-reduce(bf16[1408]{0:T(1024)(128)(2,1)S(1)} %dynamic-update-slice.8, bf16[1408]{0:T(1024)(128)(2,1)S(1)} %dynamic-update-slice.9), channel_id=1, replica_groups=mesh['fsdp'=32] {'fsdp'}, use_global_device_ids=true, to_apply=%add.8 | all-reduce | flops 2816 | bytes 11264
  509.3 93.5 %all-gather.29.cloned.1.call-done = bf16[32,44,4224]{2,1,0:T(8,128)(2,1)} async-done(((bf16[1,44,4224]{2,1,0:T(8,128)(2,1)}), bf16[32,44,4224]{2,1,0:T(8,128)(2,1)}) %all-gather.29.cloned.1.call-update) | async-done | bytes 11894800 | tf_op jit(solution)/shard_map/all_gather | solution.py:100
  617.5 110.6 %all-gather.25.cloned.1.call-done = bf16[32,44,6144]{2,1,0:T(8,128)(2,1)} async-done(((bf16[1,44,6144]{2,1,0:T(8,128)(2,1)}), bf16[32,44,6144]{2,1,0:T(8,128)(2,1)}) %all-gather.25.cloned.1.call-update) | async-done | bytes 17301520 | tf_op jit(solution)/shard_map/all_gather | solution.py:100
  747.4 99.3 %all-gather.17.cloned.1.call-done = bf16[6144,1408]{1,0:T(8,128)(2,1)} async-done(((bf16[192,1408]{1,0:T(8,128)(2,1)}), bf16[6144,1408]{1,0:T(8,128)(2,1)}) %all-gather.17.cloned.1.call-update) | async-done | bytes 17301520 | tf_op jit(solution)/shard_map/all_gather | solution.py:100
  846.7 28.5 %fusion.108 = (f32[6144]{0:T(1024)}, bf16[3,257,6144]{2,1,0:T(8,128)(2,1)}) fusion(f32[3,257,6144]{2,1,0:T(8,128)} %get-tuple-element.70, f32[6144]{0:T(1024)S(1)} %convert_element_type.166, bf16[3,257,1408]{2,1,0:T(8,128)(2,1)} %param.15, bf16[6144,1408]{1,0:T(8,128)(2,1)} %all-gather.17.cloned.1.call-done), kind=kOutput, calls=%fused_computation.139 | convolution fusion | flops 13396297728 | bytes 47943936 | tf_op jit(solution)/shard_map/bsw,fw->bsf/dot_general | solution.py:64
  875.2 23.7 %fusion.66 = (f32[1408]{0:T(1024)}, f32[3,257]{1,0:T(4,128)S(1)}, f32[3,257]{1,0:T(4,128)S(1)}, f32[1408]{0:T(1024)}, f32[3,257,1408]{2,1,0:T(8,128)S(1)}) fusion(bf16[3,257,1408]{2,1,0:T(8,128)(2,1)S(1)} %copy-done.8, f32[3,257]{1,0:T(4,128)S(1)} %add_rsqrt_fusion, f32[3,257]{1,0:T(4,128)S(1)} %broadcast_multiply_fusion.4, ...), kind=kOutput, calls=%fused_computation.86 | convolution fusion | flops 13350309888 | bytes 33318192 | tf_op jit(solution)/shard_map/bsf,wf->bsw/dot_general | solution.py:71
  928.4 29.7 %fusion.38 = f32[3,16,88,257]{3,2,1,0:T(8,128)} fusion(f32[3,16,257,257]{2,3,1,0:T(8,128)} %fusion.83, bf16[3,257,1,16,88]{4,3,2,1,0:T(8,128)(2,1)} %get-tuple-element.62, f32[3,16,257,257]{2,3,1,0:T(8,128)} %get-tuple-element.67, f32[3,16,257]{2,1,0:T(8,128)S(1)} %copy-done.15), kind=kOutput, calls=%fused_computation.50 | convolution fusion | flops 580187008 | bytes 31925568 | tf_op jit(solution)/shard_map/bhqk,bkhd->bqhd/dot_general | solution.py:83
  958.2 28.7 %fusion.35 = f32[3,16,88,257]{3,2,1,0:T(8,128)} fusion(f32[3,16,257,257]{2,3,1,0:T(8,128)} %fusion.83, bf16[3,257,1,16,88]{4,3,2,1,0:T(8,128)(2,1)S(1)} %copy-done.5, f32[3,16,257,257]{2,3,1,0:T(8,128)} %get-tuple-element.67, f32[3,16,257]{2,1,0:T(8,128)S(1)} %copy-done.15), kind=kOutput, calls=%fused_computation.49 | convolution fusion | flops 580187008 | bytes 31925568 | tf_op jit(solution)/shard_map/bhqk,bqhd->bkhd/dot_general | solution.py:84
  1043.4 21.0 convert_element_type.183
  1083.9 26.1 %convolution_bitcast_fusion = f32[6144,1408]{1,0:T(8,128)} fusion(bf16[3,257,6144]{2,1,0:T(8,128)(2,1)} %fusion.7, bf16[3,257,1408]{2,1,0:T(8,128)(2,1)} %param.15), kind=kOutput, calls=%fused_computation.4 | convolution fusion | flops 13339459584 | bytes 46248192 | tf_op jit(solution)/shard_map/bsf,bsw->fw/dot_general | solution.py:62
  1110.7 27.1 %convolution_bitcast_fusion.1 = f32[1408,6144]{1,0:T(8,128)} fusion(bf16[3,257,6144]{2,1,0:T(8,128)(2,1)} %get-tuple-element.74, bf16[3,257,1408]{2,1,0:T(8,128)(2,1)} %copy-done.7, f32[1408]{0:T(1024)S(1)} %copy-done.32, f32[1408]{0:T(1024)S(1)} %copy-done.30, f32[3,257]{1,0:T(4,128)S(1)} %copy-done.24, f32[3,257]{1,0:T(4,128)S(1)} %copy-done.19), kind=kOutput, calls=%fused_computation.5 | convolution fusion | flops 13345973248 | bytes 46265624 | tf_op jit(solution)/shard_map/bsw,bsf->wf/dot_general | solution.py:69
  1137.9 485.8 %fusion.2 = f32[48,6144]{1,0:T(8,128)S(1)} fusion(f32[1408,6144]{1,0:T(8,128)} %convolution_bitcast_fusion.1), kind=kCustom, calls=%all-reduce-scatter.2 | all-reduce-scatter fusion | flops 9437185 | bytes 35782656
  1641.6 20.2 convolution_bitcast_fusion.2
  1661.8 400.8 %fusion.104 = (f32[48,4224]{1,0:T(8,128)}, f32[48,1408]{1,0:T(8,128)}) fusion(f32[1408,4224]{1,0:T(8,128)} %convolution_bitcast_fusion.2, f32[1408,1408]{1,0:T(8,128)} %convolution_bitcast_fusion.3), kind=kCustom, calls=%all-reduce-scatter.3 | all-reduce-scatter fusion | flops 8650753 | bytes 32800768
  2111.4 20.5 collective-permute-done.2
  (217 shorter events, 393.3 us)
Async XLA Ops:
  7.2 69.5 %all-gather.21.cloned.1.call-start = ((), (), s32[]{:S(2)}) async-start(), calls=%async_computation.5 | async-start | bytes 4460544 | tf_op jit(solution)/shard_map/all_gather | solution.py:100
  9.0 167.0 %all-gather.19.cloned.1.call-start = ((), (), s32[]{:S(2)}) async-start(), calls=%async_computation.4 | async-start | bytes 13381632 | tf_op jit(solution)/shard_map/all_gather | solution.py:100
  11.0 290.3 %all-gather.23.cloned.1.call-start = ((), (), s32[]{:S(2)}) async-start(), calls=%async_computation.6 | async-start | bytes 19464192 | tf_op jit(solution)/shard_map/all_gather | solution.py:100
  13.3 406.5 %all-gather.15.cloned.1.call-start = ((), (), s32[]{:S(2)}) async-start(), calls=%async_computation.1 | async-start | bytes 17842176 | tf_op jit(solution)/shard_map/all_gather | solution.py:100
  15.4 487.9 %all-gather.27.cloned.1.call-start = ((), (), s32[]{:S(2)}) async-start(), calls=%async_computation.8 | async-start | bytes 4460544 | tf_op jit(solution)/shard_map/all_gather | solution.py:100
  66.2 125.5 %copy-start.25 = (f32[1408]{0:T(1024)}, f32[1408]{0:T(1024)S(1)}, u32[]{:S(2)}) copy-start(f32[1408]{0:T(1024)S(1)} %convert_element_type.143) | copy-start | bytes 16900
  66.3 254.4 %copy-start.29 = (f32[1408]{0:T(1024)}, f32[1408]{0:T(1024)S(1)}, u32[]{:S(2)}) copy-start(f32[1408]{0:T(1024)S(1)} %convert_element_type.160) | copy-start | bytes 16900
  66.3 254.4 %copy-start.31 = (f32[1408]{0:T(1024)}, f32[1408]{0:T(1024)S(1)}, u32[]{:S(2)}) copy-start(f32[1408]{0:T(1024)S(1)} %convert_element_type.162) | copy-start | bytes 16900
  299.0 599.9 %copy-start.18 = (f32[3,257]{1,0:T(4,128)}, f32[3,257]{1,0:T(4,128)S(1)}, u32[]{:S(2)}) copy-start(f32[3,257]{1,0:T(4,128)S(1)} %broadcast_multiply_fusion.4) | copy-start | bytes 9256
  301.1 597.7 %copy-start.23 = (f32[3,257]{1,0:T(4,128)}, f32[3,257]{1,0:T(4,128)S(1)}, u32[]{:S(2)}) copy-start(f32[3,257]{1,0:T(4,128)S(1)} %add_rsqrt_fusion) | copy-start | bytes 9256
  442.6 160.2 %all-gather.29.cloned.1.call-start = ((), (), s32[]{:S(2)}) async-start(), calls=%async_computation.9 | async-start | bytes 13381632 | tf_op jit(solution)/shard_map/all_gather | solution.py:100
  444.6 283.6 %all-gather.25.cloned.1.call-start = ((), (), s32[]{:S(2)}) async-start(), calls=%async_computation.7 | async-start | bytes 19464192 | tf_op jit(solution)/shard_map/all_gather | solution.py:100
  445.5 401.2 %all-gather.17.cloned.1.call-start = ((), (), s32[]{:S(2)}) async-start(), calls=%async_computation.2 | async-start | bytes 17842176 | tf_op jit(solution)/shard_map/all_gather | solution.py:100
  447.7 1649.2 %all-reduce.30.cloned.1.call-start = ((), (), s32[]{:S(2)}) async-start(), calls=%async_computation.10 | async-start | bytes 188416
  1083.8 1091.9 %reduce-scatter.8.cloned.1.call-start = ((), (), s32[]{:S(2)}) async-start(), calls=%async_computation.3 | async-start | bytes 35684352 | tf_op jit(solution)/shard_map/reduce_scatter | solution.py:109
  1623.7 532.1 %collective-permute-start.6 = (f32[48,6144]{1,0:T(8,128)S(1)}, f32[48,6144]{1,0:T(8,128)}, u32[]{:S(2)}, u32[]{:S(2)}) collective-permute-start(f32[48,6144]{1,0:T(8,128)S(1)} %fusion.2), channel_id=1, source_target_pairs={{0,1},{1,2},{2,3},{3,4},{4,5},{5,6},{6,7},{7,8},{8,9},{9,10},{10,1... | collective-permute-start | bytes 3538952
  1628.2 527.5 %collective-permute-start.7 = (f32[48,6144]{1,0:T(8,128)S(1)}, f32[48,6144]{1,0:T(8,128)}, u32[]{:S(2)}, u32[]{:S(2)}) collective-permute-start(f32[48,6144]{1,0:T(8,128)S(1)} %fusion.2), channel_id=1, source_target_pairs={{0,2},{1,3},{2,4},{3,5},{4,6},{5,7},{6,8},{7,9},{8,10},{9,11},{10,... | collective-permute-start | bytes 3538952
  2063.6 18.4 collective-permute-start.3
  2068.0 20.5 collective-permute-start.4
  2070.0 9.4 collective-permute-start.5
  2080.1 57.0 %collective-permute-start = (f32[48,4224]{1,0:T(8,128)}, f32[48,4224]{1,0:T(8,128)}, u32[]{:S(2)}, u32[]{:S(2)}) collective-permute-start(f32[48,4224]{1,0:T(8,128)} %get-tuple-element.58), channel_id=1, source_target_pairs={{0,1},{1,2},{2,3},{3,4},{4,5},{5,6},{6,7},{7,8},{8,9},{9,10},{10,1... | collective-permute-start | bytes 2433032
  2082.0 55.1 %collective-permute-start.1 = (f32[48,4224]{1,0:T(8,128)}, f32[48,4224]{1,0:T(8,128)}, u32[]{:S(2)}, u32[]{:S(2)}) collective-permute-start(f32[48,4224]{1,0:T(8,128)} %get-tuple-element.58), channel_id=1, source_target_pairs={{0,2},{1,3},{2,4},{3,5},{4,6},{5,7},{6,8},{7,9},{8,10},{9,11},{10,... | collective-permute-start | bytes 2433032
  2088.5 43.4 %collective-permute-start.2 = (f32[28,4224]{1,0:T(8,128)}, f32[28,4224]{1,0:T(8,128)}, u32[]{:S(2)}, u32[]{:S(2)}) collective-permute-start(f32[28,4224]{1,0:T(8,128)} %slice.15), channel_id=1, source_target_pairs={{0,3},{1,4},{2,5},{3,6},{4,7},{5,8},{6,9},{7,10},{8,11},{9,12},{10... | collective-permute-start | bytes 1419272
  2131.9 23.8 %collective-permute-start.8 = (f32[28,6144]{1,0:T(8,128)}, f32[28,6144]{1,0:T(8,128)S(1)}, u32[]{:S(2)}, u32[]{:S(2)}) collective-permute-start(f32[28,6144]{1,0:T(8,128)} %slice.17), channel_id=1, source_target_pairs={{0,3},{1,4},{2,5},{3,6},{4,7},{5,8},{6,9},{7,10},{8,11},{9,12},{10... | collective-permute-start | bytes 2064392
  (32 other events, 889.0 us)
Sparse Core Ops, SparseCore 0:
  11.5 65.1 all-gather.20
  80.2 95.8 all-gather.18
  179.5 121.8 all-gather.22
  304.7 115.0 all-gather.14
  442.7 60.5 all-gather.26
  506.6 96.1 all-gather.28
  606.3 121.8 all-gather.24
  731.7 115.0 all-gather.16
  1083.9 147.0 all-reduce.29
  1237.8 522.6 reduce-scatter.7
where the time goes:
time: 2190 us; the launch traced here: 2180 us
  blocking collectives  968 us (44%)
  waiting for transfers between devices  470 us (21%)
  matrix products  347 us (16%)
  local copies, waits for them, and re-layouts  234 us (11%)
  other arithmetic  119 us (5%)
  starting transfers between devices  29.9 us (1%)
    unnamed x4, blocking collectives  968 us
    all_gather x8, waiting for transfers between devices, gather_bf16(): lax.all_gather(shard.astype(jnp.bfloat16), 'fsdp', axis=0, tiled=True)  443 us
    unnamed x118, local copies, waits for them, and re-layouts  155 us
    convert_element_type x1, other arithmetic, forward_local(): hidden = jax.nn.gelu(pre_act, approximate=False).astype(jnp.bfloat16)  47.6 us
  transfers between devices with their start and end apart: 19, of which 10 were waited for; matrix products, arithmetic and copies ran while one was open for 61% of the time, Pallas kernels for 0%

commit v1 on v0

v1 whole, which is shorter than its diff:
```python
import math
import jax
import jax.numpy as jnp
from jax import lax
from jax.experimental import pallas as pl
from jax.experimental.pallas import tpu as pltpu
from jax.sharding import PartitionSpec as P


HEADS = 16
LN_EPS = 1e-5
DEVICES = 32
ROWS = 44
ROWS_PAD = 48
PADDED = DEVICES * ROWS_PAD
QKV = 4224
LANES = 256
SMALL_AT = (0, 1, 3, 5, 6, 7, 9, 11)
SMALL = (44, 44, 132, 44, 44, 44, 192, 44)


HEAD_DIM = 88
WIDTH = 1408


def dot_nn(left, right):
    return lax.dot_general(left, right, (((1,), (0,)), ((), ())), preferred_element_type=jnp.float32)


def dot_nt(left, right):
    return lax.dot_general(left, right, (((1,), (1,)), ((), ())), preferred_element_type=jnp.float32)


def transposed_probs(query, key):
    scores = dot_nt(key, query) * (HEAD_DIM ** -0.5)
    weights = jnp.exp(scores - jnp.max(scores, axis=0, keepdims=True))
    return weights * (1.0 / jnp.sum(weights, axis=0, keepdims=True))


def attention_fwd_kernel(qkv_ref, mixed_ref):
    for head in range(HEADS):
        query, key, value = (qkv_ref[0, :, pl.ds(part * WIDTH + head * HEAD_DIM, HEAD_DIM)] for part in range(3))
        probs = transposed_probs(query, key).astype(jnp.bfloat16)
        mixed = dot_nn(value.T, probs)
        mixed_ref[0, :, pl.ds(head * HEAD_DIM, HEAD_DIM)] = mixed.T.astype(jnp.bfloat16)


def attention_bwd_kernel(qkv_ref, grad_mixed_ref, grad_qkv_ref, bias_ref):
    for head in range(HEADS):
        query, key, value = (qkv_ref[0, :, pl.ds(part * WIDTH + head * HEAD_DIM, HEAD_DIM)] for part in range(3))
        grad_mixed = grad_mixed_ref[0, :, pl.ds(head * HEAD_DIM, HEAD_DIM)]
        probs = transposed_probs(query, key)
        grad_probs = dot_nt(value, grad_mixed)
        grad_value = dot_nn(probs.astype(jnp.bfloat16), grad_mixed)
        inner = jnp.sum(grad_probs * probs, axis=0, keepdims=True)
        grad_scores = (probs * (grad_probs - inner) * (HEAD_DIM ** -0.5)).astype(jnp.bfloat16)
        grad_key = dot_nn(grad_scores, query)
        grad_query = dot_nn(key.T, grad_scores).T
        for part, grad in enumerate((grad_query, grad_key, grad_value)):
            lanes = pl.ds(part * WIDTH + head * HEAD_DIM, HEAD_DIM)
            grad_qkv_ref[0, :, lanes] = grad.astype(jnp.bfloat16)
            bias_ref[0, :, lanes] = jnp.sum(grad, axis=0, keepdims=True)


def image_block(rows, columns):
    return pl.BlockSpec((1, rows, columns), lambda image: (image, 0, 0))


def attention_fwd(qkv):
    images, tokens, _ = qkv.shape
    return pl.pallas_call(
        attention_fwd_kernel, grid=(images,), name="attention_fwd",
        in_specs=[image_block(tokens, 3 * WIDTH)], out_specs=image_block(tokens, WIDTH),
        out_shape=jax.ShapeDtypeStruct((images, tokens, WIDTH), jnp.bfloat16),
        compiler_params=pltpu.CompilerParams(vmem_limit_bytes=40 << 20),
        cost_estimate=pl.CostEstimate(flops=6_000_000_000, bytes_accessed=9_000_000, transcendentals=3_200_000),
    )(qkv)


def attention_bwd(qkv, grad_mixed):
    images, tokens, _ = qkv.shape
    return pl.pallas_call(
        attention_bwd_kernel, grid=(images,), name="attention_bwd",
        in_specs=[image_block(tokens, 3 * WIDTH), image_block(tokens, WIDTH)],
        out_specs=[image_block(tokens, 3 * WIDTH), image_block(1, 3 * WIDTH)],
        out_shape=[jax.ShapeDtypeStruct((images, tokens, 3 * WIDTH), jnp.bfloat16),
                   jax.ShapeDtypeStruct((images, 1, 3 * WIDTH), jnp.float32)],
        compiler_params=pltpu.CompilerParams(vmem_limit_bytes=40 << 20),
        cost_estimate=pl.CostEstimate(flops=16_000_000_000, bytes_accessed=16_000_000, transcendentals=3_200_000),
    )(qkv, grad_mixed)


def layer_norm_fwd(values, gain, bias):
    mean_val = jnp.mean(values, axis=-1, keepdims=True)
    centered = values - mean_val
    inv_std = lax.rsqrt(jnp.mean(centered * centered, axis=-1, keepdims=True) + LN_EPS)
    x_hat = centered * inv_std
    return x_hat * gain + bias, x_hat, inv_std


def layer_norm_bwd(grad_norm, x_hat, inv_std, gain):
    grad_hat = grad_norm * gain
    grad_vals = inv_std * (grad_hat - jnp.mean(grad_hat, axis=-1, keepdims=True)
                           - x_hat * jnp.mean(grad_hat * x_hat, axis=-1, keepdims=True))
    return grad_vals, jnp.sum(grad_norm * x_hat, axis=(0, 1)), jnp.sum(grad_norm, axis=(0, 1))


def forward_local(full, tokens):
    (ln1_gain, ln1_bias, qkv_weight, qkv_bias, out_weight, out_bias,
     ln2_gain, ln2_bias, fc_weight, fc_bias, proj_weight, proj_bias) = full
    resid = tokens.astype(jnp.float32)
    normed, hat_one, inv_one = layer_norm_fwd(resid, ln1_gain, ln1_bias)
    normed_one = normed.astype(jnp.bfloat16)
    qkv_vals = (jnp.einsum("bsw,wk->bsk", normed_one, qkv_weight, preferred_element_type=jnp.float32) + qkv_bias).astype(jnp.bfloat16)
    mixed = attention_fwd(qkv_vals)
    middle = (resid + jnp.einsum("bsw,wv->bsv", mixed, out_weight, preferred_element_type=jnp.float32) + out_bias).astype(jnp.bfloat16)
    middle_wide = middle.astype(jnp.float32)
    normed, hat_two, inv_two = layer_norm_fwd(middle_wide, ln2_gain, ln2_bias)
    normed_two = normed.astype(jnp.bfloat16)
    pre_act = jnp.einsum("bsw,wf->bsf", normed_two, fc_weight, preferred_element_type=jnp.float32) + fc_bias
    hidden = jax.nn.gelu(pre_act, approximate=False).astype(jnp.bfloat16)
    resid_out = (middle_wide + jnp.einsum("bsf,fw->bsw", hidden, proj_weight, preferred_element_type=jnp.float32) + proj_bias).astype(jnp.bfloat16)
    saved = (hat_one, inv_one, normed_one, qkv_vals, mixed, hat_two, inv_two, normed_two, pre_act, hidden)
    return resid_out, saved


def pad_rows(values):
    width = values.shape[-1]
    source = lax.broadcasted_iota(jnp.int32, (width, PADDED), 0)
    target = lax.broadcasted_iota(jnp.int32, (width, PADDED), 1)
    spread = (source // ROWS * ROWS_PAD + source % ROWS == target).astype(jnp.bfloat16)
    return jnp.einsum("bsw,wp->bsp", values, spread, preferred_element_type=jnp.float32).astype(jnp.bfloat16)


def backward_local(weights, saved, grad_out):
    (ln1_gain, qkv_weight, out_weight, ln2_gain, fc_weight, proj_weight) = weights
    (hat_one, inv_one, normed_one, qkv_vals, mixed, hat_two, inv_two, normed_two, pre_act, hidden) = saved
    grad_wide = grad_out.astype(jnp.float32)
    d_proj_weight = jnp.einsum("bsf,bsw->fw", hidden, grad_out, preferred_element_type=jnp.float32)
    d_proj_weight, grad_out = lax.optimization_barrier((d_proj_weight, grad_out))
    d_proj_bias = jnp.sum(grad_wide, axis=(0, 1))
    grad_hidden = jnp.einsum("bsw,fw->bsf", grad_out, proj_weight, preferred_element_type=jnp.float32)
    gauss_cdf = 0.5 * (1.0 + lax.erf(pre_act * (0.5 ** 0.5)))
    gauss_pdf = jnp.exp(-0.5 * pre_act * pre_act) * ((2.0 * math.pi) ** -0.5)
    grad_pre = grad_hidden * (gauss_cdf + pre_act * gauss_pdf)
    grad_pre_low = grad_pre.astype(jnp.bfloat16)
    d_fc_weight = jnp.einsum("bsw,bsf->wf", pad_rows(normed_two), grad_pre_low, preferred_element_type=jnp.float32)
    d_fc_weight, grad_pre_low = lax.optimization_barrier((d_fc_weight, grad_pre_low))
    d_fc_bias = jnp.sum(grad_pre, axis=(0, 1))
    grad_norm = jnp.einsum("bsf,wf->bsw", grad_pre_low, fc_weight, preferred_element_type=jnp.float32)
    grad_ln, d_ln2_gain, d_ln2_bias = layer_norm_bwd(grad_norm, hat_two, inv_two, ln2_gain)
    grad_middle = grad_wide + grad_ln
    grad_middle_low = grad_middle.astype(jnp.bfloat16)
    d_out_weight = jnp.einsum("bsw,bsv->wv", pad_rows(mixed), grad_middle_low, preferred_element_type=jnp.float32)
    d_out_weight, grad_middle_low = lax.optimization_barrier((d_out_weight, grad_middle_low))
    d_out_bias = jnp.sum(grad_middle, axis=(0, 1))
    grad_mixed = jnp.einsum("bsv,wv->bsw", grad_middle_low, out_weight, preferred_element_type=jnp.float32)
    grad_qkv_low, bias_parts = attention_bwd(qkv_vals, grad_mixed.astype(jnp.bfloat16))
    d_qkv_weight = jnp.einsum("bsw,bsk->wk", pad_rows(normed_one), grad_qkv_low, preferred_element_type=jnp.float32)
    d_qkv_bias = jnp.sum(bias_parts, axis=(0, 1))
    grad_norm = jnp.einsum("bsk,wk->bsw", grad_qkv_low, qkv_weight, preferred_element_type=jnp.float32)
    grad_ln, d_ln1_gain, d_ln1_bias = layer_norm_bwd(grad_norm, hat_one, inv_one, ln1_gain)
    grad_in = (grad_middle + grad_ln).astype(jnp.bfloat16)
    return grad_in, (d_ln1_gain, d_ln1_bias, d_qkv_weight, d_qkv_bias, d_out_weight, d_out_bias,
                     d_ln2_gain, d_ln2_bias, d_fc_weight, d_fc_bias, d_proj_weight, d_proj_bias)


def solution(mesh):
    specs = (P("fsdp"),) * 14

    def gather(shard):
        return lax.all_gather(shard, "fsdp", axis=0, tiled=True)

    def pad_shard(shard):
        return jnp.pad(shard, ((0, ROWS_PAD - ROWS), (0, 0)))

    def unpad(padded):
        columns = padded.shape[1]
        return padded.reshape(DEVICES, ROWS_PAD, columns)[:, :ROWS].reshape(DEVICES * ROWS, columns)

    def device_step(resid_in, grad_out, *shards):
        low = [shard.astype(jnp.bfloat16) for shard in shards]
        (_, _, qkv_weight, _, out_weight, _,
         _, _, fc_weight, _, proj_weight, _) = low
        small = jnp.concatenate([jnp.pad(shards[index][None], ((0, 0), (0, LANES - size)))
                                 for index, size in zip(SMALL_AT, SMALL)], axis=0).astype(jnp.bfloat16)
        both = jnp.concatenate([pad_shard(qkv_weight), pad_shard(out_weight),
                                jnp.pad(small, ((0, ROWS_PAD - len(SMALL)), (0, 0)))], axis=1)
        both_full = gather(both)
        fc_shard, proj_shard = pad_shard(fc_weight), proj_weight
        fc_full = unpad(gather(fc_shard))
        proj_full = gather(proj_shard)
        small_full = both_full[:, -LANES:].reshape(DEVICES, ROWS_PAD, LANES)
        pieces = [small_full[:, row, :size].reshape(DEVICES * size) for row, size in enumerate(SMALL)]
        g1, b1, bqkv, bout, g2, b2, bfc, bproj = pieces
        qkv_full = unpad(both_full[:, :QKV])
        out_full = unpad(both_full[:, QKV:-LANES])
        full = (g1, b1, qkv_full, bqkv, out_full, bout, g2, b2, fc_full, bfc, proj_full, bproj)
        resid_out, saved = forward_local(full, resid_in)
        weights = (g1, qkv_full, out_full, g2, fc_full, proj_full)
        grad_in, grads = backward_local(weights, saved, grad_out)
        (d_g1, d_b1, d_qkv, d_bqkv, d_out, d_bout, d_g2, d_b2, d_fc, d_bfc, d_proj, d_bproj) = grads

        def scatter(grad):
            return lax.psum_scatter(grad, "fsdp", scatter_dimension=0, tiled=True)

        proj_part = scatter(d_proj)
        fc_part = scatter(d_fc)[:ROWS]
        out_part = scatter(d_out)[:ROWS]
        qkv_part = scatter(d_qkv)[:ROWS]
        packed = jnp.concatenate([jnp.pad(grad.reshape(DEVICES, 1, size), ((0, 0), (0, 0), (0, LANES - size)))
                                  for grad, size in zip((d_g1, d_b1, d_bqkv, d_bout, d_g2, d_b2, d_bfc, d_bproj), SMALL)], axis=1)
        small_sums = jnp.sum(lax.all_to_all(packed, "fsdp", split_axis=0, concat_axis=0, tiled=True), axis=0)
        small_parts = [small_sums[row, :size] for row, size in enumerate(SMALL)]
        s_g1, s_b1, s_bqkv, s_bout, s_g2, s_b2, s_bfc, s_bproj = small_parts
        return (resid_out, grad_in, s_g1, s_b1, qkv_part, s_bqkv, out_part, s_bout,
                s_g2, s_b2, fc_part, s_bfc, proj_part, s_bproj)

    return jax.shard_map(device_step, mesh=mesh, in_specs=specs, out_specs=specs, check_vma=False)
```

time: 2190 us -> 1570 us (0.72)
  blocking collectives: 968 us -> 0 us
  waiting for transfers between devices: 470 us -> 1110 us
  local copies, waits for them, and re-layouts: 234 us -> 78.8 us
  matrix products: 347 us -> 236 us
  other arithmetic: 119 us -> 67.1 us
  Pallas kernels: 0 us -> 47.8 us
  starting transfers between devices: 29.9 us -> 3.02 us
    unnamed x4 -> x0, blocking collectives: 968 us -> none
    reduce_scatter x1 -> x4, waiting for transfers between devices: 0.01 us -> 962 us  [scatter(): return lax.psum_scatter(grad, 'fsdp', scatter_dimension=0, tiled=True)]
    all_gather x8 -> x3, waiting for transfers between devices: 443 us -> 150 us  [gather(): return lax.all_gather(shard, 'fsdp', axis=0, tiled=True)]
    unnamed x118 -> x82, local copies, waits for them, and re-layouts: 155 us -> 15.4 us
    dot_general x9 -> x6, matrix products: 168 us -> 67.2 us  [the longest x1 24.6 us: backward_local(): jnp.einsum('bsw,bsf->wf', pad_rows(normed_two), grad_pre_low, preferred_e...]
    pallas_call x0 -> x2, Pallas kernels: none -> 47.8 us  [the longest x1 29 us: attention_bwd(): pl.pallas_call(attention_bwd_kernel, grid=(images,), name='attention_bwd'...]
    unnamed x10 -> x0, starting transfers between devices: 29.6 us -> none
    unnamed x20 -> x7, waiting for transfers between devices: 26.9 us -> 1.3 us
  transfers between devices with their start and end apart: 19 -> 8, of which waited for: 10 -> 6; matrix products, arithmetic and copies ran while one was open for 61% -> 18% of each run, Pallas kernels for 0% -> 3%
where the time goes in v1:
time: 1570 us; the launch traced here: 1560 us
  waiting for transfers between devices  1110 us (71%)
  matrix products  236 us (15%)
  local copies, waits for them, and re-layouts  78.8 us (5%)
  other arithmetic  67.1 us (4%)
  Pallas kernels  47.8 us (3%)
    reduce_scatter x4, waiting for transfers between devices, scatter(): return lax.psum_scatter(grad, 'fsdp', scatter_dimension=0, tiled=True)  962 us
    all_gather x3, waiting for transfers between devices, gather(): return lax.all_gather(shard, 'fsdp', axis=0, tiled=True)  150 us
    convert_element_type x1, other arithmetic, forward_local(): hidden = jax.nn.gelu(pre_act, approximate=False).astype(jnp.bfloat16)  46.8 us
    reshape x3, local copies, waits for them, and re-layouts, unpad(): padded.reshape(DEVICES, ROWS_PAD, columns)[:, :ROWS]  41.1 us
  transfers between devices with their start and end apart: 8, of which 6 were waited for; matrix products, arithmetic and copies ran while one was open for 18% of the time, Pallas kernels for 3%

profile of v1, /device:TPU:1, one launch (start us, length us, event | category | flops | bytes accessed | tf_op | source)
XLA Modules:
  0.0 1562.0 jit_solution(5175982156551705867)
XLA Ops:
  21.7 117.2 %all-gather.4.cloned.1.call-done = bf16[1536,5888]{1,0:T(8,128)(2,1)} async-done(((bf16[48,5888]{1,0:T(8,128)(2,1)}), bf16[1536,5888]{1,0:T(8,128)(2,1)}) %all-gather.4.cloned.1.call-update) | async-done | bytes 18087952 | tf_op jit(solution)/shard_map/all_gather | solution.py:172
  141.8 10.9 slice.103
  152.7 15.7 %reshape.192 = bf16[1408,4224,1]{1,0,2:T(8,128)(2,1)} reshape(bf16[32,44,4224]{2,1,0:T(8,128)(2,1)} %bitcast.88) | data formatting | bytes 23789568 | tf_op jit(solution)/shard_map/reshape | solution.py:179
  173.0 6.0 reshape.193
  179.0 15.7 %add_convert_fusion.qkv_ref = bf16[3,257,4224]{2,1,0:T(8,128)(2,1)S(1)} fusion(bf16[1408,4224,1]{1,0,2:T(8,128)(2,1)} %reshape.192, f32[4224]{0:T(1024)S(1)} %reshape.186, bf16[3,257,1408]{2,1,0:T(8,128)(2,1)S(1)} %copy-done.3, f32[1408]{0:T(1024)S(1)} %reshape.185, f32[1408]{0:T(1024)S(1)} %reshape.184, f32[3,257]{1,0:T(4,128)S(1)} %add_rsqrt_fusion.1, ...), kind=kOutput, calls=%fused_computation.35 | convolution fusion | flops 9183904768 | bytes 20613656 | tf_op jit(solution)/shard_map/bsw,wk->bsk/dot_general | solution.py:114
  194.8 18.8 %attention_fwd.1 = bf16[3,257,1408]{2,1,0:T(8,128)(2,1)S(1)} custom-call(bf16[3,257,4224]{2,1,0:T(8,128)(2,1)S(1)} %add_convert_fusion.qkv_ref), custom_call_target="tpu_custom_call" | custom-call | flops 6000000000 | bytes 9000000 | tf_op jit(solution)/shard_map/attention_fwd/pallas_call | solution.py:71
  225.0 6.4 convolution_convert_fusion.3
  231.4 33.2 %all-gather.6.cloned.1.call-done = bf16[1536,6144]{1,0:T(8,128)(2,1)} async-done(((bf16[48,6144]{1,0:T(8,128)(2,1)}), bf16[1536,6144]{1,0:T(8,128)(2,1)}) %all-gather.6.cloned.1.call-update) | async-done | bytes 18874384 | tf_op jit(solution)/shard_map/all_gather | solution.py:172
  264.6 19.4 %reshape.194 = bf16[1408,6144,1]{1,0,2:T(8,128)(2,1)} reshape(bf16[32,44,6144]{2,1,0:T(8,128)(2,1)} %bitcast.91) | data formatting | bytes 34603008 | tf_op jit(solution)/shard_map/reshape | solution.py:179
  284.0 29.8 %fusion.32 = (u8[257,6144]{1,0:T(8,128)(4,1)S(1)}, u8[257,6144]{1,0:T(8,128)(4,1)S(1)}, f32[3,257,6144]{2,1,0:T(8,128)}) fusion(f32[6144]{0:T(1024)S(1)} %reshape.190, bf16[1408,6144,1]{1,0,2:T(8,128)(2,1)} %reshape.194, bf16[3,257,1408]{2,1,0:T(8,128)(2,1)S(1)} %copy-done.7, f32[1408]{0:T(1024)S(1)} %reshape.189, f32[1408]{0:T(1024)S(1)} %reshape.188, ...), kind=kOutput, calls=%fused_computation.60 | convolution fusion | flops 13409133568 | bytes 41620760 | tf_op jit(solution)/shard_map/bsw,wf->bsf/dot_general | solution.py:120
  313.9 46.8 %fusion.2 = bf16[3,257,6144]{2,1,0:T(8,128)(2,1)S(1)} fusion(f32[3,257,6144]{2,1,0:T(8,128)} %get-tuple-element.59, f32[6144]{0:T(1024)S(1)} %reshape.190, u8[257,6144]{1,0:T(8,128)(4,1)S(1)} %get-tuple-element.31, u8[257,6144]{1,0:T(8,128)(4,1)S(1)} %get-tuple-element.30), kind=kLoop, calls=%fused_computation.7 | loop fusion | flops 336328704 | bytes 31604736 | tf_op jit(solution)/shard_map/convert_element_type | solution.py:121
  364.3 24.1 %convolution_bitcast_fusion.1 = f32[6144,1408]{1,0:T(8,128)} fusion(bf16[3,257,6144]{2,1,0:T(8,128)(2,1)S(1)} %fusion.2, bf16[3,257,1408]{2,1,0:T(8,128)(2,1)S(1)} %copy-done.11), kind=kOutput, calls=%fused_computation.3 | convolution fusion | flops 13339459584 | bytes 46248192 | tf_op jit(solution)/shard_map/bsf,bsw->fw/dot_general | solution.py:139
  388.4 25.9 %fusion.84 = (f32[6144]{0:T(1024)S(1)}, bf16[3,257,6144]{2,1,0:T(8,128)(2,1)S(1)}) fusion(f32[3,257,6144]{2,1,0:T(8,128)} %get-tuple-element.59, f32[6144]{0:T(1024)S(1)} %reshape.190, bf16[3,257,1408]{2,1,0:T(8,128)(2,1)} %param.15, bf16[6144,1408]{1,0:T(8,128)(2,1)} %all-gather.8.cloned.1.call-done), kind=kOutput, calls=%fused_computation.144 | convolution fusion | flops 13396297728 | bytes 47943936 | tf_op jit(solution)/shard_map/bsw,fw->bsf/dot_general | solution.py:142
  417.9 24.6 %convolution_bitcast_fusion = f32[1536,6144]{1,0:T(8,128)} fusion(bf16[3,257,1536]{2,1,0:T(8,128)(2,1)S(1)} %copy-done.38, bf16[3,257,6144]{2,1,0:T(8,128)(2,1)S(1)} %get-tuple-element.23), kind=kOutput, calls=%fused_computation.2 | convolution fusion | flops 14552137728 | bytes 49591296 | tf_op jit(solution)/shard_map/bsw,bsf->wf/dot_general | solution.py:147
  442.5 23.2 %fusion.38 = (f32[1408]{0:T(1024)S(1)}, f32[3,257]{1,0:T(4,128)S(1)}, f32[3,257]{1,0:T(4,128)S(1)}, f32[1408]{0:T(1024)S(1)}, f32[3,257,1408]{2,1,0:T(8,128)S(1)}) fusion(bf16[3,257,1408]{2,1,0:T(8,128)(2,1)S(1)} %copy-done.7, f32[3,257]{1,0:T(4,128)S(1)} %add_rsqrt_fusion, f32[3,257]{1,0:T(4,128)S(1)} %broadcast_multiply_fusion.4, f32[1408]{0:T(1024)S(1)} %reshape.188, ...), kind=kOutput, calls=%fused_computation.66 | convolution fusion | flops 13350309888 | bytes 33318192 | tf_op jit(solution)/shard_map/bsf,wf->bsw/dot_general | solution.py:150
  472.1 7.9 convolution_bitcast_fusion.3
  491.1 29.0 %attention_bwd.1 = (bf16[3,257,4224]{2,1,0:T(8,128)(2,1)S(1)}, f32[3,1,4224]{2,1,0:T(1,128)S(1)}) custom-call(bf16[3,257,4224]{2,1,0:T(8,128)(2,1)} %copy-done.1, bf16[3,257,1408]{2,1,0:T(8,128)(2,1)S(1)} %convolution_convert_fusion.grad_mixed_ref), custom_call_target="tpu_custom_call" | custom-call | flops 16000000000 | bytes 16000000 | tf_op jit(solution)/shard_map/attention_bwd/pallas_call | solution.py:82
  522.9 17.7 %convolution_bitcast_fusion.2 = f32[1536,4224]{1,0:T(8,128)} fusion(bf16[3,257,1536]{2,1,0:T(8,128)(2,1)S(1)} %convolution_convert_fusion.1, bf16[3,257,4224]{2,1,0:T(8,128)(2,1)S(1)} %get-tuple-element.25), kind=kOutput, calls=%fused_computation.4 | convolution fusion | flops 10004594688 | bytes 34834176 | tf_op jit(solution)/shard_map/bsw,bsk->wk/dot_general | solution.py:159
  542.9 18.4 %fusion.47 = (f32[1408]{0:T(1024)S(1)}, f32[3,257]{1,0:T(4,128)S(1)}, f32[3,257]{1,0:T(4,128)S(1)}, f32[1408]{0:T(1024)S(1)}, f32[3,257,1408]{2,1,0:T(8,128)}) fusion(bf16[3,257,1408]{2,1,0:T(8,128)(2,1)S(1)} %copy-done.4, f32[3,257]{1,0:T(4,128)S(1)} %copy-done.21, f32[3,257]{1,0:T(4,128)S(1)} %copy-done.17, f32[1408]{0:T(1024)S(1)} %copy-done.19, ...), kind=kOutput, calls=%fused_computation.75 | convolution fusion | flops 9181728768 | bytes 24950832 | tf_op jit(solution)/shard_map/bsk,wk->bsw/dot_general | solution.py:161
  565.6 22.5 %fusion.52 = bf16[3,257,1408]{2,1,0:T(8,128)(2,1)} fusion(bf16[3,257,1408]{2,1,0:T(8,128)(2,1)} %copy-done.6, bf16[3,257,6144]{2,1,0:T(8,128)(2,1)} %copy-done.5, bf16[6144,1408]{1,0:T(8,128)(2,1)} %all-gather.8.cloned.1.call-done, f32[1408]{0:T(1024)S(1)} %reshape.191), kind=kOutput, calls=%fused_computation.80 | convolution fusion | flops 13343801344 | bytes 31123456 | tf_op jit(solution)/shard_map/bsf,fw->bsw/dot_general | solution.py:122
  592.5 16.6 %reduce-scatter.7.cloned.1.call-done = f32[48,1408]{1,0:T(8,128)} async-done(((f32[1536,1408]{1,0:T(8,128)}), f32[48,1408]{1,0:T(8,128)}) %reduce-scatter.7.cloned.1.call-update) | async-done | bytes 270352 | tf_op jit(solution)/shard_map/reduce_scatter | solution.py:205
  609.1 256.3 %reduce-scatter.5.cloned.1.call-done = f32[48,4224]{1,0:T(8,128)} async-done(((f32[1536,4224]{1,0:T(8,128)}), f32[48,4224]{1,0:T(8,128)}) %reduce-scatter.5.cloned.1.call-update) | async-done | bytes 811024 | tf_op jit(solution)/shard_map/reduce_scatter | solution.py:205
  865.4 334.4 %reduce-scatter.11.cloned.1.call-done = f32[192,1408]{1,0:T(8,128)} async-done(((f32[6144,1408]{1,0:T(8,128)}), f32[192,1408]{1,0:T(8,128)}) %reduce-scatter.11.cloned.1.call-update) | async-done | bytes 1081360 | tf_op jit(solution)/shard_map/reduce_scatter | solution.py:205
  1199.7 355.2 %reduce-scatter.9.cloned.1.call-done = f32[48,6144]{1,0:T(8,128)} async-done(((f32[1536,6144]{1,0:T(8,128)}), f32[48,6144]{1,0:T(8,128)}) %reduce-scatter.9.cloned.1.call-update) | async-done | bytes 1179664 | tf_op jit(solution)/shard_map/reduce_scatter | solution.py:205
  (181 shorter events, 71.2 us)
Async XLA Ops:
  7.2 131.7 %all-gather.4.cloned.1.call-start = ((), (), s32[]{:S(2)}) async-start(), calls=%async_computation.5 | async-start | bytes 18653184 | tf_op jit(solution)/shard_map/all_gather | solution.py:172
  15.8 248.7 %all-gather.6.cloned.1.call-start = ((), (), s32[]{:S(2)}) async-start(), calls=%async_computation.6 | async-start | bytes 19464192 | tf_op jit(solution)/shard_map/all_gather | solution.py:172
  18.1 370.3 %all-gather.8.cloned.1.call-start = ((), (), s32[]{:S(2)}) async-start(), calls=%async_computation.7 | async-start | bytes 17842176 | tf_op jit(solution)/shard_map/all_gather | solution.py:172
  20.3 588.8 %reduce-scatter.7.cloned.1.call-start = ((), (), s32[]{:S(2)}) async-start(), calls=%async_computation.9 | async-start | bytes 8921088 | tf_op jit(solution)/shard_map/reduce_scatter | solution.py:205
  20.4 204.6 %copy-start.32 = (pred[1408]{0:T(1024)(128)(4,1)}, pred[1408]{0:T(1024)(128)(4,1)S(1)}, u32[]{:S(2)}) copy-start(pred[1408]{0:T(1024)(128)(4,1)S(1)} %get-tuple-element.66) | copy-start | bytes 4228
  20.4 204.6 %copy-start.34 = (pred[1408]{0:T(1024)(128)(4,1)}, pred[1408]{0:T(1024)(128)(4,1)S(1)}, u32[]{:S(2)}) copy-start(pred[1408]{0:T(1024)(128)(4,1)S(1)} %get-tuple-element.67) | copy-start | bytes 4228
  20.4 204.6 %copy-start.24 = (s32[1408]{0:T(1024)}, s32[1408]{0:T(1024)S(1)}, u32[]{:S(2)}) copy-start(s32[1408]{0:T(1024)S(1)} %get-tuple-element.64) | copy-start | bytes 16900
  20.4 204.6 %copy-start.26 = (s32[1408]{0:T(1024)}, s32[1408]{0:T(1024)S(1)}, u32[]{:S(2)}) copy-start(s32[1408]{0:T(1024)S(1)} %get-tuple-element.65) | copy-start | bytes 16900
  20.4 204.6 %copy-start.28 = (s32[1408]{0:T(1024)}, s32[1408]{0:T(1024)S(1)}, u32[]{:S(2)}) copy-start(s32[1408]{0:T(1024)S(1)} %get-tuple-element.62) | copy-start | bytes 16900
  20.4 204.6 %copy-start.30 = (s32[1408]{0:T(1024)}, s32[1408]{0:T(1024)S(1)}, u32[]{:S(2)}) copy-start(s32[1408]{0:T(1024)S(1)} %get-tuple-element.63) | copy-start | bytes 16900
  20.9 158.1 %copy-start.16 = (f32[3,257]{1,0:T(4,128)}, f32[3,257]{1,0:T(4,128)S(1)}, u32[]{:S(2)}) copy-start(f32[3,257]{1,0:T(4,128)S(1)} %broadcast_multiply_fusion.5) | copy-start | bytes 9256
  21.7 157.3 %copy-start.20 = (f32[3,257]{1,0:T(4,128)}, f32[3,257]{1,0:T(4,128)S(1)}, u32[]{:S(2)}) copy-start(f32[3,257]{1,0:T(4,128)S(1)} %add_rsqrt_fusion.1) | copy-start | bytes 9256
  141.5 37.5 %copy-start.18 = (f32[1408]{0:T(1024)}, f32[1408]{0:T(1024)S(1)}, u32[]{:S(2)}) copy-start(f32[1408]{0:T(1024)S(1)} %reshape.184) | copy-start | bytes 16900
  141.7 37.3 %copy-start.22 = (f32[1408]{0:T(1024)}, f32[1408]{0:T(1024)S(1)}, u32[]{:S(2)}) copy-start(f32[1408]{0:T(1024)S(1)} %reshape.185) | copy-start | bytes 16900
  313.8 50.5 %copy-start.11 = (bf16[3,257,1408]{2,1,0:T(8,128)(2,1)S(1)}, bf16[3,257,1408]{2,1,0:T(8,128)(2,1)}, u32[]{:S(2)}) copy-start(bf16[3,257,1408]{2,1,0:T(8,128)(2,1)} %param.15) | copy-start | bytes 6513412
  388.4 29.5 %copy-start.38 = (bf16[3,257,1536]{2,1,0:T(8,128)(2,1)S(1)}, bf16[3,257,1536]{2,1,0:T(8,128)(2,1)}, u32[]{:S(2)}) copy-start(bf16[3,257,1536]{2,1,0:T(8,128)(2,1)} %convolution_convert_fusion.3) | copy-start | bytes 7105540
  442.5 23.2 %copy-start.12 = (bf16[3,257,1408]{2,1,0:T(8,128)(2,1)S(1)}, bf16[3,257,1408]{2,1,0:T(8,128)(2,1)}, u32[]{:S(2)}) copy-start(bf16[3,257,1408]{2,1,0:T(8,128)(2,1)} %param.15) | copy-start | bytes 6513412
  480.1 385.2 %reduce-scatter.5.cloned.1.call-start = ((), (), s32[]{:S(2)}) async-start(), calls=%async_computation.8 | async-start | bytes 26763264 | tf_op jit(solution)/shard_map/reduce_scatter | solution.py:205
  540.7 659.1 %reduce-scatter.11.cloned.1.call-start = ((), (), s32[]{:S(2)}) async-start(), calls=%async_computation.11 | async-start | bytes 35684352 | tf_op jit(solution)/shard_map/reduce_scatter | solution.py:205
  541.3 1013.6 %reduce-scatter.9.cloned.1.call-start = ((), (), s32[]{:S(2)}) async-start(), calls=%async_computation.10 | async-start | bytes 38928384 | tf_op jit(solution)/shard_map/reduce_scatter | solution.py:205
  542.9 45.2 %slice-start = ((s8[4460544]{0:T(1024)(128)(4,1)}), s8[266240]{0:T(1024)(128)(4,1)S(1)}, s32[]{:S(2)}) async-start(s8[4460544]{0:T(1024)(128)(4,1)} %bitcast.89), calls=%async_computation.12 | async-start | bytes 532480
  562.8 27.9 %all-to-all-start = ((f32[32,8,256]{2,1,0:T(8,128)}), f32[32,8,256]{2,1,0:T(8,128)S(1)}, u32[]{:S(2)}, u32[]{:S(2)}) async-start(f32[32,8,256]{2,1,0:T(8,128)} %concatenate.12), calls=%async_computation | async-start | bytes 524288 | tf_op jit(solution)/shard_map/all_to_all | solution.py:213
  565.6 22.5 %slice-start.1 = ((s8[4460544]{0:T(1024)(128)(4,1)}), s8[4194304]{0:T(1024)(128)(4,1)S(1)}, s32[]{:S(2)}) async-start(s8[4460544]{0:T(1024)(128)(4,1)} %bitcast.89), calls=%async_computation.13 | async-start | bytes 8388608
  565.6 22.5 %copy-start.8 = (f32[3,257,1408]{2,1,0:T(8,128)S(1)}, f32[3,257,1408]{2,1,0:T(8,128)}, u32[]{:S(2)}) copy-start(f32[3,257,1408]{2,1,0:T(8,128)} %get-tuple-element.61) | copy-start | bytes 13026820
  (25 other events, 123.2 us)
Sparse Core Ops, SparseCore 0:
  16.0 122.8 all-gather.3
  142.4 122.1 all-gather.5
  268.1 115.0 all-gather.7
  480.2 128.8 reduce-scatter.6
  615.9 249.3 reduce-scatter.4
  872.2 327.4 reduce-scatter.10
  1206.7 348.1 reduce-scatter.8

commit v2 on v1

--- a/solution.py
+++ b/solution.py
@@ -12,7 +12,7 @@
 DEVICES = 32
 ROWS = 44
 ROWS_PAD = 48
-PADDED = DEVICES * ROWS_PAD
+HALF = DEVICES // 2 * ROWS_PAD
 QKV = 4224
 LANES = 256
 SMALL_AT = (0, 1, 3, 5, 6, 7, 9, 11)
@@ -124,19 +124,45 @@
     return resid_out, saved
 
 
-def pad_rows(values):
+def core_of_chip():
+    return lax.axis_index("fsdp") % 2
+
+
+def swap(values):
+    return lax.ppermute(values, "fsdp", [(device, device ^ 1) for device in range(DEVICES)])
+
+
+def split_columns(values, block, block_pad):
     width = values.shape[-1]
-    source = lax.broadcasted_iota(jnp.int32, (width, PADDED), 0)
-    target = lax.broadcasted_iota(jnp.int32, (width, PADDED), 1)
-    spread = (source // ROWS * ROWS_PAD + source % ROWS == target).astype(jnp.bfloat16)
-    return jnp.einsum("bsw,wp->bsp", values, spread, preferred_element_type=jnp.float32).astype(jnp.bfloat16)
+    source = lax.broadcasted_iota(jnp.int32, (width, 2 * HALF), 0)
+    target = lax.broadcasted_iota(jnp.int32, (width, 2 * HALF), 1)
+    chunk = source // block
+    place = chunk // 2 * block_pad + source % block + jnp.where(chunk % 2 == core_of_chip(), 0, HALF)
+    spread = (place == target).astype(jnp.bfloat16)
+    both = jnp.einsum("bsw,wp->bsp", values, spread, preferred_element_type=jnp.float32).astype(jnp.bfloat16)
+    return both[..., :HALF], both[..., HALF:]
+
+
+def chip_product(left, left_other, right, right_other):
+    own = jnp.einsum("bsm,bsn->mn", left, right, preferred_element_type=jnp.float32)
+    return own + jnp.einsum("bsm,bsn->mn", left_other, right_other, preferred_element_type=jnp.float32)
+
+
+def rows_gradient(inputs, grads):
+    mine, theirs = split_columns(inputs, ROWS, ROWS_PAD)
+    return chip_product(mine, swap(theirs), grads, swap(grads))
+
+
+def columns_gradient(inputs, grads):
+    mine, theirs = split_columns(grads, WIDTH // 2, HALF)
+    return chip_product(inputs, swap(inputs), mine, swap(theirs))
 
 
 def backward_local(weights, saved, grad_out):
     (ln1_gain, qkv_weight, out_weight, ln2_gain, fc_weight, proj_weight) = weights
     (hat_one, inv_one, normed_one, qkv_vals, mixed, hat_two, inv_two, normed_two, pre_act, hidden) = saved
     grad_wide = grad_out.astype(jnp.float32)
-    d_proj_weight = jnp.einsum("bsf,bsw->fw", hidden, grad_out, preferred_element_type=jnp.float32)
+    d_proj_weight = columns_gradient(hidden, grad_out)
     d_proj_weight, grad_out = lax.optimization_barrier((d_proj_weight, grad_out))
     d_proj_bias = jnp.sum(grad_wide, axis=(0, 1))
     grad_hidden = jnp.einsum("bsw,fw->bsf", grad_out, proj_weight, preferred_element_type=jnp.float32)
@@ -144,19 +170,19 @@
     gauss_pdf = jnp.exp(-0.5 * pre_act * pre_act) * ((2.0 * math.pi) ** -0.5)
     grad_pre = grad_hidden * (gauss_cdf + pre_act * gauss_pdf)
     grad_pre_low = grad_pre.astype(jnp.bfloat16)
-    d_fc_weight = jnp.einsum("bsw,bsf->wf", pad_rows(normed_two), grad_pre_low, preferred_element_type=jnp.float32)
+    d_fc_weight = rows_gradient(normed_two, grad_pre_low)
     d_fc_weight, grad_pre_low = lax.optimization_barrier((d_fc_weight, grad_pre_low))
     d_fc_bias = jnp.sum(grad_pre, axis=(0, 1))
     grad_norm = jnp.einsum("bsf,wf->bsw", grad_pre_low, fc_weight, preferred_element_type=jnp.float32)
     grad_ln, d_ln2_gain, d_ln2_bias = layer_norm_bwd(grad_norm, hat_two, inv_two, ln2_gain)
     grad_middle = grad_wide + grad_ln
     grad_middle_low = grad_middle.astype(jnp.bfloat16)
-    d_out_weight = jnp.einsum("bsw,bsv->wv", pad_rows(mixed), grad_middle_low, preferred_element_type=jnp.float32)
+    d_out_weight = rows_gradient(mixed, grad_middle_low)
     d_out_weight, grad_middle_low = lax.optimization_barrier((d_out_weight, grad_middle_low))
     d_out_bias = jnp.sum(grad_middle, axis=(0, 1))
     grad_mixed = jnp.einsum("bsv,wv->bsw", grad_middle_low, out_weight, preferred_element_type=jnp.float32)
     grad_qkv_low, bias_parts = attention_bwd(qkv_vals, grad_mixed.astype(jnp.bfloat16))
-    d_qkv_weight = jnp.einsum("bsw,bsk->wk", pad_rows(normed_one), grad_qkv_low, preferred_element_type=jnp.float32)
+    d_qkv_weight = rows_gradient(normed_one, grad_qkv_low)
     d_qkv_bias = jnp.sum(bias_parts, axis=(0, 1))
     grad_norm = jnp.einsum("bsk,wk->bsw", grad_qkv_low, qkv_weight, preferred_element_type=jnp.float32)
     grad_ln, d_ln1_gain, d_ln1_bias = layer_norm_bwd(grad_norm, hat_one, inv_one, ln1_gain)
@@ -202,9 +228,15 @@
         (d_g1, d_b1, d_qkv, d_bqkv, d_out, d_bout, d_g2, d_b2, d_fc, d_bfc, d_proj, d_bproj) = grads
 
         def scatter(grad):
-            return lax.psum_scatter(grad, "fsdp", scatter_dimension=0, tiled=True)
+            groups = [list(range(core, DEVICES, 2)) for core in range(2)]
+            return lax.psum_scatter(grad, "fsdp", scatter_dimension=0, tiled=True, axis_index_groups=groups)
 
         proj_part = scatter(d_proj)
+        core, proj_rows = core_of_chip(), proj_part.shape[0] // 2
+        mine = lax.dynamic_slice_in_dim(proj_part, core * proj_rows, proj_rows)
+        theirs = swap(lax.dynamic_slice_in_dim(proj_part, (1 - core) * proj_rows, proj_rows))
+        proj_part = jnp.concatenate([jnp.where(core == 0, mine, theirs)[:, :WIDTH // 2],
+                                     jnp.where(core == 0, theirs, mine)[:, :WIDTH // 2]], axis=1)
         fc_part = scatter(d_fc)[:ROWS]
         out_part = scatter(d_out)[:ROWS]
         qkv_part = scatter(d_qkv)[:ROWS]

time: 1570 us -> 1350 us (0.86)
  waiting for transfers between devices: 1110 us -> 853 us
  matrix products: 236 us -> 275 us
    reduce_scatter x4, waiting for transfers between devices: 962 us -> 691 us  [scatter(): lax.psum_scatter(grad, 'fsdp', scatter_dimension=0, tiled=True, axis_inde...]
    dot_general x7 -> x12, matrix products: 91.3 us -> 127 us  [the longest x4 61.7 us: chip_product(): jnp.einsum('bsm,bsn->mn', left_other, right_other, preferred_element_type...]
  transfers between devices with their start and end apart: 8 -> 17, of which waited for: 6 -> 7; matrix products, arithmetic and copies ran while one was open for 18% -> 30% of each run, Pallas kernels for 3% -> 4%
where the time goes in v2:
time: 1350 us; the launch traced here: 1340 us
  waiting for transfers between devices  853 us (63%)
  matrix products  275 us (20%)
  other arithmetic  74.4 us (6%)
  local copies, waits for them, and re-layouts  69.3 us (5%)
  Pallas kernels  49.8 us (4%)
  between operations  15.1 us (1%)
    reduce_scatter x4, waiting for transfers between devices, scatter(): lax.psum_scatter(grad, 'fsdp', scatter_dimension=0, tiled=True, axis_inde...  691 us
    all_gather x3, waiting for transfers between devices, gather(): return lax.all_gather(shard, 'fsdp', axis=0, tiled=True)  161 us
    dot_general x4, matrix products, chip_product(): jnp.einsum('bsm,bsn->mn', left_other, right_other, preferred_element_type...  61.7 us
    convert_element_type x1, other arithmetic, forward_local(): hidden = jax.nn.gelu(pre_act, approximate=False).astype(jnp.bfloat16)  47.8 us
    dot_general x4, matrix products, chip_product(): jnp.einsum('bsm,bsn->mn', left, right, preferred_element_type=jnp.float32)  43.8 us
    reshape x3, local copies, waits for them, and re-layouts, unpad(): padded.reshape(DEVICES, ROWS_PAD, columns)[:, :ROWS]  41.1 us
    pallas_call x1, Pallas kernels, attention_bwd(): pl.pallas_call(attention_bwd_kernel, grid=(images,), name='attention_bwd'...  31 us
    dot_general x1, matrix products, forward_local(): jnp.einsum('bsw,wf->bsf', normed_two, fc_weight, preferred_element_type=j...  29.4 us
  transfers between devices with their start and end apart: 17, of which 7 were waited for; matrix products, arithmetic and copies ran while one was open for 30% of the time, Pallas kernels for 4%

profile of v2, /device:TPU:1, one launch (start us, length us, event | category | flops | bytes accessed | tf_op | source)
XLA Modules:
  0.0 1343.0 jit_solution(1171310262362743941)
XLA Ops:
  21.6 117.3 %all-gather.4.cloned.1.call-done = bf16[1536,5888]{1,0:T(8,128)(2,1)} async-done(((bf16[48,5888]{1,0:T(8,128)(2,1)}), bf16[1536,5888]{1,0:T(8,128)(2,1)}) %all-gather.4.cloned.1.call-update) | async-done | bytes 18087952 | tf_op jit(solution)/shard_map/all_gather | solution.py:198
  141.3 11.0 slice.143
  152.3 15.7 %reshape.192 = bf16[1408,4224,1]{1,0,2:T(8,128)(2,1)} reshape(bf16[32,44,4224]{2,1,0:T(8,128)(2,1)} %bitcast.109) | data formatting | bytes 23789568 | tf_op jit(solution)/shard_map/reshape | solution.py:205
  179.1 15.7 %add_convert_fusion.qkv_ref = bf16[3,257,4224]{2,1,0:T(8,128)(2,1)S(1)} fusion(bf16[1408,4224,1]{1,0,2:T(8,128)(2,1)} %reshape.192, f32[4224]{0:T(1024)S(1)} %reshape.186, bf16[3,257,1408]{2,1,0:T(8,128)(2,1)S(1)} %copy-done.4, f32[1408]{0:T(1024)S(1)} %reshape.185, f32[1408]{0:T(1024)S(1)} %reshape.184, f32[3,257]{1,0:T(4,128)S(1)} %add_rsqrt_fusion.1, ...), kind=kOutput, calls=%fused_computation.42 | convolution fusion | flops 9183904768 | bytes 20613656 | tf_op jit(solution)/shard_map/bsw,wk->bsk/dot_general | solution.py:114
  194.9 18.8 %attention_fwd.1 = bf16[3,257,1408]{2,1,0:T(8,128)(2,1)S(1)} custom-call(bf16[3,257,4224]{2,1,0:T(8,128)(2,1)S(1)} %add_convert_fusion.qkv_ref), custom_call_target="tpu_custom_call" | custom-call | flops 6000000000 | bytes 9000000 | tf_op jit(solution)/shard_map/attention_fwd/pallas_call | solution.py:71
  220.9 43.7 %all-gather.6.cloned.1.call-done = bf16[1536,6144]{1,0:T(8,128)(2,1)} async-done(((bf16[48,6144]{1,0:T(8,128)(2,1)}), bf16[1536,6144]{1,0:T(8,128)(2,1)}) %all-gather.6.cloned.1.call-update) | async-done | bytes 18874384 | tf_op jit(solution)/shard_map/all_gather | solution.py:198
  264.6 19.4 %reshape.194 = bf16[1408,6144,1]{1,0,2:T(8,128)(2,1)} reshape(bf16[32,44,6144]{2,1,0:T(8,128)(2,1)} %bitcast.110) | data formatting | bytes 34603008 | tf_op jit(solution)/shard_map/reshape | solution.py:205
  284.0 29.4 %fusion.58 = (u8[257,6144]{1,0:T(8,128)(4,1)S(1)}, u8[257,6144]{1,0:T(8,128)(4,1)S(1)}, f32[3,257,6144]{2,1,0:T(8,128)}) fusion(f32[6144]{0:T(1024)S(1)} %reshape.190, bf16[1408,6144,1]{1,0,2:T(8,128)(2,1)} %reshape.194, bf16[3,257,1408]{2,1,0:T(8,128)(2,1)S(1)} %copy-done.7, f32[1408]{0:T(1024)S(1)} %reshape.189, f32[1408]{0:T(1024)S(1)} %reshape.188, ...), kind=kOutput, calls=%fused_computation.99 | convolution fusion | flops 13409133568 | bytes 41620760 | tf_op jit(solution)/shard_map/bsw,wf->bsf/dot_general | solution.py:120
  313.4 47.8 %fusion.2 = bf16[3,257,6144]{2,1,0:T(8,128)(2,1)} fusion(f32[3,257,6144]{2,1,0:T(8,128)} %get-tuple-element.61, f32[6144]{0:T(1024)S(1)} %reshape.190, u8[257,6144]{1,0:T(8,128)(4,1)S(1)} %get-tuple-element.31, u8[257,6144]{1,0:T(8,128)(4,1)S(1)} %get-tuple-element.30), kind=kLoop, calls=%fused_computation.12 | loop fusion | flops 336328704 | bytes 31604736 | tf_op jit(solution)/shard_map/convert_element_type | solution.py:121
  368.5 16.8 %fusion.112 = f32[6144,768,1]{1,0,2:T(8,128)} fusion(bf16[3,257,6144]{2,1,0:T(8,128)(2,1)} %fusion.2, bf16[3,257,1536]{2,1,0:T(8,128)(2,1)S(1)} %fusion.105), kind=kOutput, calls=%fused_computation.147 | convolution fusion | flops 7276068864 | bytes 29564928 | tf_op jit(solution)/shard_map/bsm,bsn->mn/dot_general | solution.py:147
  385.3 21.6 %bitcast_add_fusion.1 = f32[6144,768]{1,0:T(8,128)} fusion(f32[6144,768,1]{1,0,2:T(8,128)} %fusion.112, bf16[3,257,6144]{2,1,0:T(8,128)(2,1)} %collective-permute-done, bf16[3,257,768]{2,1,0:T(8,128)(2,1)S(1)} %collective-permute-done.1), kind=kOutput, calls=%fused_computation.37 | convolution fusion | flops 7280787456 | bytes 48407040 | tf_op jit(solution)/shard_map/bsm,bsn->mn/dot_general | solution.py:148
  407.0 26.6 %fusion.154 = (f32[6144]{0:T(1024)}, bf16[3,257,6144]{2,1,0:T(8,128)(2,1)S(1)}) fusion(f32[3,257,6144]{2,1,0:T(8,128)} %get-tuple-element.61, f32[6144]{0:T(1024)S(1)} %reshape.190, bf16[3,257,1408]{2,1,0:T(8,128)(2,1)} %param.15, bf16[6144,1408]{1,0:T(8,128)(2,1)} %all-gather.8.cloned.1.call-done), kind=kOutput, calls=%fused_computation.223 | convolution fusion | flops 13396297728 | bytes 47943936 | tf_op jit(solution)/shard_map/bsw,fw->bsf/dot_general | solution.py:168
  439.6 13.7 %fusion.114 = f32[768,6144,1]{1,0,2:T(8,128)} fusion(bf16[3,257,6144]{2,1,0:T(8,128)(2,1)S(1)} %get-tuple-element.23, bf16[3,257,1536]{2,1,0:T(8,128)(2,1)S(1)} %fusion.96), kind=kOutput, calls=%fused_computation.149 | convolution fusion | flops 7276068864 | bytes 29822976 | tf_op jit(solution)/shard_map/bsm,bsn->mn/dot_general | solution.py:147
  453.4 22.3 %bitcast_add_fusion = f32[768,6144]{1,0:T(8,128)} fusion(f32[768,6144,1]{1,0,2:T(8,128)} %fusion.114, bf16[3,257,768]{2,1,0:T(8,128)(2,1)S(1)} %collective-permute-done.2, bf16[3,257,6144]{2,1,0:T(8,128)(2,1)} %collective-permute-done.3), kind=kOutput, calls=%fused_computation.36 | convolution fusion | flops 7280787456 | bytes 48407040 | tf_op jit(solution)/shard_map/bsm,bsn->mn/dot_general | solution.py:148
  475.7 23.6 %fusion.64 = (f32[1408]{0:T(1024)S(1)}, f32[3,257]{1,0:T(4,128)S(1)}, f32[3,257]{1,0:T(4,128)S(1)}, f32[1408]{0:T(1024)S(1)}, f32[3,257,1408]{2,1,0:T(8,128)S(1)}) fusion(bf16[3,257,1408]{2,1,0:T(8,128)(2,1)S(1)} %copy-done.7, f32[3,257]{1,0:T(4,128)S(1)} %add_rsqrt_fusion, f32[3,257]{1,0:T(4,128)S(1)} %broadcast_multiply_fusion.4, ...), kind=kOutput, calls=%fused_computation.105 | convolution fusion | flops 13350309888 | bytes 33318192 | tf_op jit(solution)/shard_map/bsf,wf->bsw/dot_general | solution.py:176
  523.3 31.0 %attention_bwd.1 = (bf16[3,257,4224]{2,1,0:T(8,128)(2,1)}, f32[3,1,4224]{2,1,0:T(1,128)S(1)}) custom-call(bf16[3,257,4224]{2,1,0:T(8,128)(2,1)} %copy-done, bf16[3,257,1408]{2,1,0:T(8,128)(2,1)S(1)} %convolution_convert_fusion.grad_mixed_ref), custom_call_target="tpu_custom_call" | custom-call | flops 16000000000 | bytes 16000000 | tf_op jit(solution)/shard_map/attention_bwd/pallas_call | solution.py:82
  560.5 10.6 fusion.108
  571.1 13.4 %bitcast_add_fusion.2 = f32[768,4224]{1,0:T(8,128)} fusion(f32[768,4224,1]{1,0,2:T(8,128)S(1)} %fusion.108, bf16[3,257,768]{2,1,0:T(8,128)(2,1)S(1)} %collective-permute-done.6, bf16[3,257,4224]{2,1,0:T(8,128)(2,1)} %collective-permute-done.7), kind=kOutput, calls=%fused_computation.51 | convolution fusion | flops 5005541376 | bytes 33649920 | tf_op jit(solution)/shard_map/bsm,bsn->mn/dot_general | solution.py:148
  585.5 22.5 %fusion.78 = bf16[3,257,1408]{2,1,0:T(8,128)(2,1)} fusion(bf16[3,257,1408]{2,1,0:T(8,128)(2,1)} %copy-done.6, bf16[3,257,6144]{2,1,0:T(8,128)(2,1)} %fusion.2, bf16[6144,1408]{1,0:T(8,128)(2,1)} %all-gather.8.cloned.1.call-done, f32[1408]{0:T(1024)S(1)} %reshape.191), kind=kOutput, calls=%fused_computation.119 | convolution fusion | flops 13343801344 | bytes 31123456 | tf_op jit(solution)/shard_map/bsf,fw->bsw/dot_general | solution.py:122
  608.7 18.1 %fusion.73 = (f32[1408]{0:T(1024)S(1)}, f32[3,257]{1,0:T(4,128)S(1)}, f32[3,257]{1,0:T(4,128)S(1)}, f32[1408]{0:T(1024)S(1)}, f32[3,257,1408]{2,1,0:T(8,128)}) fusion(bf16[3,257,1408]{2,1,0:T(8,128)(2,1)S(1)} %copy-done.5, f32[3,257]{1,0:T(4,128)S(1)} %copy-done.17, f32[3,257]{1,0:T(4,128)S(1)} %copy-done.13, f32[1408]{0:T(1024)S(1)} %copy-done.15, ...), kind=kOutput, calls=%fused_computation.114 | convolution fusion | flops 9181728768 | bytes 24950832 | tf_op jit(solution)/shard_map/bsk,wk->bsw/dot_general | solution.py:187
  631.5 57.3 %reduce-scatter.11.cloned.1.call-done = f32[384,768]{1,0:T(8,128)} async-done(((f32[6144,768]{1,0:T(8,128)}), f32[384,768]{1,0:T(8,128)}) %reduce-scatter.11.cloned.1.call-update) | async-done | bytes 1179664 | tf_op jit(solution)/shard_map/reduce_scatter | solution.py:232
  702.8 128.2 %reduce-scatter.7.cloned.1.call-done = f32[48,1408]{1,0:T(8,128)} async-done(((f32[768,1408]{1,0:T(8,128)}), f32[48,1408]{1,0:T(8,128)}) %reduce-scatter.7.cloned.1.call-update) | async-done | bytes 270352 | tf_op jit(solution)/shard_map/reduce_scatter | solution.py:232
  831.0 214.7 %reduce-scatter.5.cloned.1.call-done = f32[48,4224]{1,0:T(8,128)} async-done(((f32[768,4224]{1,0:T(8,128)}), f32[48,4224]{1,0:T(8,128)}) %reduce-scatter.5.cloned.1.call-update) | async-done | bytes 811024 | tf_op jit(solution)/shard_map/reduce_scatter | solution.py:232
  1045.6 290.3 %reduce-scatter.9.cloned.1.call-done = f32[48,6144]{1,0:T(8,128)} async-done(((f32[768,6144]{1,0:T(8,128)}), f32[48,6144]{1,0:T(8,128)}) %reduce-scatter.9.cloned.1.call-update) | async-done | bytes 1179664 | tf_op jit(solution)/shard_map/reduce_scatter | solution.py:232
  (175 shorter events, 98.2 us)
Async XLA Ops:
  7.2 131.7 %all-gather.4.cloned.1.call-start = ((), (), s32[]{:S(2)}) async-start(), calls=%async_computation.5 | async-start | bytes 18653184 | tf_op jit(solution)/shard_map/all_gather | solution.py:198
  15.9 248.7 %all-gather.6.cloned.1.call-start = ((), (), s32[]{:S(2)}) async-start(), calls=%async_computation.6 | async-start | bytes 19464192 | tf_op jit(solution)/shard_map/all_gather | solution.py:198
  18.1 388.9 %all-gather.8.cloned.1.call-start = ((), (), s32[]{:S(2)}) async-start(), calls=%async_computation.7 | async-start | bytes 17842176 | tf_op jit(solution)/shard_map/all_gather | solution.py:198
  20.3 668.6 %reduce-scatter.11.cloned.1.call-start = ((), (), s32[]{:S(2)}) async-start(), calls=%async_computation.11 | async-start | bytes 20054016 | tf_op jit(solution)/shard_map/reduce_scatter | solution.py:232
  20.8 158.3 %copy-start.12 = (f32[3,257]{1,0:T(4,128)}, f32[3,257]{1,0:T(4,128)S(1)}, u32[]{:S(2)}) copy-start(f32[3,257]{1,0:T(4,128)S(1)} %broadcast_multiply_fusion.5) | copy-start | bytes 9256
  21.6 157.5 %copy-start.16 = (f32[3,257]{1,0:T(4,128)}, f32[3,257]{1,0:T(4,128)S(1)}, u32[]{:S(2)}) copy-start(f32[3,257]{1,0:T(4,128)S(1)} %add_rsqrt_fusion.1) | copy-start | bytes 9256
  140.9 38.1 %copy-start.14 = (f32[1408]{0:T(1024)}, f32[1408]{0:T(1024)S(1)}, u32[]{:S(2)}) copy-start(f32[1408]{0:T(1024)S(1)} %reshape.184) | copy-start | bytes 16900
  141.0 38.0 %copy-start.19 = (f32[1408]{0:T(1024)}, f32[1408]{0:T(1024)S(1)}, u32[]{:S(2)}) copy-start(f32[1408]{0:T(1024)S(1)} %reshape.185) | copy-start | bytes 16900
  361.3 24.0 %collective-permute-start = (bf16[3,257,6144]{2,1,0:T(8,128)(2,1)}, bf16[3,257,6144]{2,1,0:T(8,128)(2,1)}, u32[]{:S(2)}, u32[]{:S(2)}) collective-permute-start(bf16[3,257,6144]{2,1,0:T(8,128)(2,1)} %fusion.2), channel_id=1, source_target_pairs={{0,1},{1,0},{2,3},{3,2},{4,5},{5,4},{6,7},{7,6},{8,9},{9,8},{10,11... | collective-permute-start | bytes 28422152 | tf_op jit(solution)/shard_map/ppermute | solution.py:132
  368.4 16.9 %collective-permute-start.1 = (bf16[3,257,768]{2,1,0:T(8,128)(2,1)S(1)}, bf16[3,257,768]{2,1,0:T(8,128)(2,1)S(1)}, u32[]{:S(2)}, u32[]{:S(2)}) collective-permute-start(bf16[3,257,768]{2,1,0:T(8,128)(2,1)S(1)} %slice.156), channel_id=1, source_target_pairs={{0,1},{1,0},{2,3},{3,2},{4,5},{5,4},{6,7},{7,6},{8,9},{9,8},{10,11... | collective-permute-start | bytes 3552776 | tf_op jit(solution)/shard_map/ppermute | solution.py:132
  407.0 424.0 %reduce-scatter.7.cloned.1.call-start = ((), (), s32[]{:S(2)}) async-start(), calls=%async_computation.9 | async-start | bytes 4595712 | tf_op jit(solution)/shard_map/reduce_scatter | solution.py:232
  433.6 19.7 %collective-permute-start.3 = (bf16[3,257,6144]{2,1,0:T(8,128)(2,1)S(1)}, bf16[3,257,6144]{2,1,0:T(8,128)(2,1)}, u32[]{:S(2)}, u32[]{:S(2)}) collective-permute-start(bf16[3,257,6144]{2,1,0:T(8,128)(2,1)S(1)} %get-tuple-element.23), channel_id=1, source_target_pairs={{0,1},{1,0},{2,3},{3,2},{4,5},{5,4},{6,7},{7,6},{8,9},{9,8},{10,11... | collective-permute-start | bytes 28422152 | tf_op jit(solution)/shard_map/ppermute | solution.py:132
  439.6 13.8 %collective-permute-start.2 = (bf16[3,257,768]{2,1,0:T(8,128)(2,1)S(1)}, bf16[3,257,768]{2,1,0:T(8,128)(2,1)S(1)}, u32[]{:S(2)}, u32[]{:S(2)}) collective-permute-start(bf16[3,257,768]{2,1,0:T(8,128)(2,1)S(1)} %slice.157), channel_id=1, source_target_pairs={{0,1},{1,0},{2,3},{3,2},{4,5},{5,4},{6,7},{7,6},{8,9},{9,8},{10,11... | collective-permute-start | bytes 3552776 | tf_op jit(solution)/shard_map/ppermute | solution.py:132
  504.3 8.4 collective-permute-start.5
  509.8 3.0 collective-permute-start.4
  523.2 31.6 %copy-start.5 = (bf16[3,257,1408]{2,1,0:T(8,128)(2,1)S(1)}, bf16[3,257,1408]{2,1,0:T(8,128)(2,1)}, u32[]{:S(2)}) copy-start(bf16[3,257,1408]{2,1,0:T(8,128)(2,1)} %param.14) | copy-start | bytes 6513412
  523.2 31.6 %copy-start.13 = (f32[3,257]{1,0:T(4,128)S(1)}, f32[3,257]{1,0:T(4,128)}, u32[]{:S(2)}) copy-start(f32[3,257]{1,0:T(4,128)} %copy-done.12) | copy-start | bytes 9256
  523.2 31.6 %copy-start.15 = (f32[1408]{0:T(1024)S(1)}, f32[1408]{0:T(1024)}, u32[]{:S(2)}) copy-start(f32[1408]{0:T(1024)} %copy-done.14) | copy-start | bytes 16900
  554.3 16.9 %collective-permute-start.7 = (bf16[3,257,4224]{2,1,0:T(8,128)(2,1)}, bf16[3,257,4224]{2,1,0:T(8,128)(2,1)}, u32[]{:S(2)}, u32[]{:S(2)}) collective-permute-start(bf16[3,257,4224]{2,1,0:T(8,128)(2,1)} %get-tuple-element.25), channel_id=1, source_target_pairs={{0,1},{1,0},{2,3},{3,2},{4,5},{5,4},{6,7},{7,6},{8,9},{9,8},{10,11... | collective-permute-start | bytes 19540232 | tf_op jit(solution)/shard_map/ppermute | solution.py:132
  554.6 491.0 %reduce-scatter.5.cloned.1.call-start = ((), (), s32[]{:S(2)}) async-start(), calls=%async_computation.8 | async-start | bytes 13787136 | tf_op jit(solution)/shard_map/reduce_scatter | solution.py:232
  560.3 10.8 collective-permute-start.6
  584.6 751.3 %reduce-scatter.9.cloned.1.call-start = ((), (), s32[]{:S(2)}) async-start(), calls=%async_computation.10 | async-start | bytes 20054016 | tf_op jit(solution)/shard_map/reduce_scatter | solution.py:232
  628.4 69.3 %all-to-all-start = ((f32[32,8,256]{2,1,0:T(8,128)}), f32[32,8,256]{2,1,0:T(8,128)}, u32[]{:S(2)}, u32[]{:S(2)}) async-start(f32[32,8,256]{2,1,0:T(8,128)} %concatenate.15), calls=%async_computation | async-start | bytes 524288 | tf_op jit(solution)/shard_map/all_to_all | solution.py:245
  690.9 9.5 collective-permute-start.8
  (15 other events, 212.2 us)
Sparse Core Ops, SparseCore 0:
  16.0 122.8 all-gather.3
  142.4 122.1 all-gather.5
  268.1 116.5 all-gather.7
  407.1 281.7 reduce-scatter.10
  694.4 136.4 reduce-scatter.6
  837.1 208.4 reduce-scatter.4
  1052.0 283.9 reduce-scatter.8
